TPU v7x, 32 devices: a whole 2x2x4 slice. The times are simulated.
32 devices in a mesh: replica: 16 (over z, x, core), shard: 2 (over y).
Axes of the slice: x: 2, y: 2, z: 4, core: 2. Of those that a mesh axis runs over, the one named last changes fastest.
Arguments:
- tokens: bfloat16 [16, 2, 512, 768], P('replica', None, 'shard'), may hold values from -6 to 6
- cotangent: bfloat16 [16, 2, 512, 768], P('replica', None, 'shard'), may hold values from -6 to 6
- seq_units: int32 [16, 2], P('replica'), may hold values from 0 to 2, as said below
- deal: int32 [16, 2], P('replica'), may hold values from 0 to 1, as said below
- timesteps: int32 [16, 2], P('replica'), may hold values from 0 to 999
- ln_gain: bfloat16 [768], P('shard'), may hold values from 0.5 to 1.5
- ln_bias: bfloat16 [768], P('shard'), may hold values from -2 to 2
- qkv_weight: bfloat16 [768, 2304], P('shard'), may hold values from -0.21875 to 0.21875
- qkv_bias: bfloat16 [2304], P('shard'), may hold values from -2 to 2
- out_weight: bfloat16 [768, 768], P('shard'), may hold values from -2.5 to 2.5
- out_bias: bfloat16 [768], P('shard'), may hold values from -2 to 2
- ada_weight: bfloat16 [128, 2304], P('shard'), may hold values from -0.5 to 0.5
- ada_bias: bfloat16 [2304], P('shard'), may hold values from -3 to 3
- up_weight: bfloat16 [768, 3072], P('shard'), may hold values from -0.21875 to 0.21875
- up_bias: bfloat16 [3072], P('shard'), may hold values from -2 to 2
- down_weight: bfloat16 [3072, 768], P('shard'), may hold values from -0.109375 to 0.109375
- down_bias: bfloat16 [768], P('shard'), may hold values from -2 to 2
Outputs:
- mixed: bfloat16 [16, 2, 512, 768], P('replica', None, 'shard')
- held: bfloat16 [16, 2, 1024, 768], P('replica', 'shard')
- grad_tokens: bfloat16 [16, 2, 512, 768], P('replica', None, 'shard')
- grad_ln_gain: float32 [768], P('shard')
- grad_ln_bias: float32 [768], P('shard')
- grad_qkv_weight: float32 [768, 2304], P('shard')
- grad_qkv_bias: float32 [2304], P('shard')
- grad_out_weight: float32 [768, 768], P('shard')
- grad_out_bias: float32 [768], P('shard')
- grad_ada_weight: float32 [128, 2304], P('shard')
- grad_ada_bias: float32 [2304], P('shard')
- grad_up_weight: float32 [768, 3072], P('shard')
- grad_up_bias: float32 [3072], P('shard')
- grad_down_weight: float32 [3072, 768], P('shard')
- grad_down_bias: float32 [768], P('shard')
Inputs may be any that keep to these rules, and one draw needn't show every extreme that they name: `seq_units`: each row lists the group's sequences in the order in which they lie; an entry is 1 or 2 units for a used sequence and 0 for an unused one, and unused entries may stand anywhere in the row; a row sums to 2, and at least one sequence of every row has 2 units. Each row is a permutation of the 2 owners of a group; sequence j goes to owner deal[g, j], and owners named by unused entries receive nothing, so an owner receives at most one sequence. `timesteps`: entries of unused sequences are not read.
All inputs are finite; a program needn't handle non-finite values.
Results may differ from a plain program's by a relative error of at most 0.019.
Values may be sent and summed in bfloat16 or wider, within the bound.
A program may use at most 192 MiB of HBM per device.

v0:
```python
import math

import jax
import jax.numpy as jnp
from jax import lax
from jax.sharding import PartitionSpec as P

HEADS = 12


EPSILON = 1e-05
NEGATIVE = -1000000000.0
HIGHEST = lax.Precision.HIGHEST


def normalize(values):
    center = values - jnp.mean(values, axis=-1, keepdims=True)
    spread = jnp.mean(center * center, axis=-1, keepdims=True)
    inverse = lax.rsqrt(spread + EPSILON)
    return (center * inverse, inverse)


def normalize_back(grad, normed, inverse):
    return inverse * (
        grad
        - jnp.mean(grad, axis=-1, keepdims=True)
        - normed * jnp.mean(grad * normed, axis=-1, keepdims=True)
    )


def rotary_tables(length, head_dim):
    half = head_dim // 2
    freqs = jnp.exp(-math.log(10000.0) * jnp.arange(half, dtype=jnp.float32) / half)
    angles = jnp.arange(length, dtype=jnp.float32)[:, None] * freqs[None, :]
    return (jnp.cos(angles)[:, None, :], jnp.sin(angles)[:, None, :])


def rotate(field, cosines, sines):
    half = field.shape[-1] // 2
    first = field[..., :half]
    second = field[..., half:]
    return jnp.concatenate(
        [first * cosines - second * sines, second * cosines + first * sines], axis=-1
    )


def unrotate(grad, cosines, sines):
    half = grad.shape[-1] // 2
    first = grad[..., :half]
    second = grad[..., half:]
    return jnp.concatenate(
        [first * cosines + second * sines, second * cosines - first * sines], axis=-1
    )


def time_features(step, width):
    half = width // 2
    freqs = jnp.exp(-math.log(10000.0) * jnp.arange(half, dtype=jnp.float32) / half)
    angles = step.astype(jnp.float32) * freqs
    return jnp.concatenate([jnp.cos(angles), jnp.sin(angles)])


def inner_rows(left, right):
    return lax.dot_general(
        left, right, (((0,), (0,)), ((), ())), preferred_element_type=jnp.float32
    )


def times_transposed(left, right):
    return lax.dot_general(
        left, right, (((1,), (1,)), ((), ())), preferred_element_type=jnp.float32
    )


def on_device(
    tokens,
    cotangent,
    seq_units,
    deal,
    timesteps,
    ln_gain,
    ln_bias,
    qkv_weight,
    qkv_bias,
    out_weight,
    out_bias,
    ada_weight,
    ada_bias,
    up_weight,
    up_bias,
    down_weight,
    down_bias,
):
    owners = lax.axis_size("shard")
    myself = lax.axis_index("shard")
    unit_count = tokens.shape[1]
    piece_rows = tokens.shape[2]
    width = tokens.shape[3]
    length = 2 * owners * piece_rows
    block_rows = min(512, length)
    head_count = HEADS
    head_dim = width // head_count
    factor = 1.0 / math.sqrt(head_dim)
    units = seq_units[0]
    dealt = deal[0]
    step_list = timesteps[0]
    starts = jnp.cumsum(units) - units
    unit_ids = jnp.arange(unit_count, dtype=jnp.int32)
    member = (
        (unit_ids[None, :] >= starts[:, None]) & (unit_ids[None, :] < (starts + units)[:, None])
    ).astype(jnp.int32)
    target = jnp.sum(member * dealt[:, None], axis=0)
    place = jnp.sum(member * (unit_ids[None, :] - starts[:, None]), axis=0)
    select = (
        (place[None, None, :] == jnp.arange(2, dtype=jnp.int32)[:, None, None])
        & (target[None, None, :] == jnp.arange(owners, dtype=jnp.int32)[None, :, None])
    ).astype(jnp.bfloat16)
    owned = (dealt == myself) & (units > 0)
    own_units = jnp.sum(jnp.where(owned, units, 0))
    own_step = jnp.sum(jnp.where(owned, step_list, 0))
    key_live = jnp.arange(length, dtype=jnp.int32) < own_units * (owners * piece_rows)

    def deal_rows(local):
        return jnp.einsum(
            "pqk,ktd->pqtd", select, local, preferred_element_type=jnp.float32
        ).astype(jnp.bfloat16)

    def collect_rows(arrived):
        return jnp.einsum(
            "pqk,pqtd->ktd", select, arrived, preferred_element_type=jnp.float32
        ).astype(jnp.bfloat16)[None]

    arrived_rows = lax.all_to_all(
        deal_rows(tokens[0]), "shard", split_axis=1, concat_axis=1, tiled=True
    )
    rows = arrived_rows.reshape(length, width).astype(jnp.float32)
    (
        gain,
        norm_shift,
        qkv_full,
        qkv_add,
        out_full,
        out_add,
        ada_full,
        ada_add,
        up_full,
        up_add,
        down_full,
        down_add,
    ) = (
        lax.all_gather(ln_gain, "shard", axis=0, tiled=True),
        lax.all_gather(ln_bias, "shard", axis=0, tiled=True),
        lax.all_gather(qkv_weight, "shard", axis=0, tiled=True),
        lax.all_gather(qkv_bias, "shard", axis=0, tiled=True),
        lax.all_gather(out_weight, "shard", axis=0, tiled=True),
        lax.all_gather(out_bias, "shard", axis=0, tiled=True),
        lax.all_gather(ada_weight, "shard", axis=0, tiled=True),
        lax.all_gather(ada_bias, "shard", axis=0, tiled=True),
        lax.all_gather(up_weight, "shard", axis=0, tiled=True),
        lax.all_gather(up_bias, "shard", axis=0, tiled=True),
        lax.all_gather(down_weight, "shard", axis=0, tiled=True),
        lax.all_gather(down_bias, "shard", axis=0, tiled=True),
    )
    normed_first, inverse_first = normalize(rows)
    normed_in = (normed_first * gain + norm_shift).astype(jnp.bfloat16)
    projected = jnp.dot(normed_in, qkv_full, preferred_element_type=jnp.float32) + qkv_add
    cosines, sines = rotary_tables(length, head_dim)
    queries = (
        rotate(projected[:, :width].reshape(length, head_count, head_dim), cosines, sines)
        .astype(jnp.bfloat16)
        .transpose(1, 0, 2)
    )
    key_rows = (
        rotate(
            projected[:, width : 2 * width].reshape(length, head_count, head_dim), cosines, sines
        )
        .astype(jnp.bfloat16)
        .transpose(1, 0, 2)
    )
    value_rows = (
        projected[:, 2 * width :]
        .reshape(length, head_count, head_dim)
        .astype(jnp.bfloat16)
        .transpose(1, 0, 2)
    )

    def attend(items):
        query_head, key_head, value_head = items
        outputs = []
        totals = []
        for offset in range(0, length, block_rows):
            query_block = query_head[offset : offset + block_rows]
            scores = (
                jnp.einsum("qd,kd->qk", query_block, key_head, preferred_element_type=jnp.float32)
                * factor
            )
            scores = jnp.where(key_live[None, :], scores, NEGATIVE)
            highest = jnp.max(scores, axis=1, keepdims=True)
            expon = jnp.exp(scores - highest)
            summed = jnp.sum(expon, axis=1, keepdims=True)
            probs = (expon / summed).astype(jnp.bfloat16)
            outputs.append(jnp.dot(probs, value_head, preferred_element_type=jnp.float32))
            totals.append((highest + jnp.log(summed))[:, 0])
        return (jnp.concatenate(outputs, axis=0), jnp.concatenate(totals, axis=0))

    heads_out, log_totals = lax.map(attend, (queries, key_rows, value_rows))
    attended = heads_out.transpose(1, 0, 2).reshape(length, width).astype(jnp.bfloat16)
    middle = rows + jnp.dot(attended, out_full, preferred_element_type=jnp.float32) + out_add
    features = time_features(own_step, ada_full.shape[0])
    modulation = (
        jnp.dot(
            features[None, :],
            ada_full.astype(jnp.float32),
            precision=HIGHEST,
            preferred_element_type=jnp.float32,
        )[0]
        + ada_add
    )
    shift = modulation[:width]
    scale = modulation[width : 2 * width]
    gate = modulation[2 * width :]
    normed_second, inverse_second = normalize(middle)
    modulated = (normed_second * (1.0 + scale) + shift).astype(jnp.bfloat16)
    hidden_pre = jnp.dot(modulated, up_full, preferred_element_type=jnp.float32) + up_add
    hidden = jax.nn.gelu(hidden_pre).astype(jnp.bfloat16)
    result = jnp.dot(hidden, down_full, preferred_element_type=jnp.float32) + down_add
    output_rows = (middle + gate * result).astype(jnp.bfloat16)
    held = jnp.where(key_live[:, None], output_rows, jnp.zeros_like(output_rows))[None, None]
    mixed = collect_rows(
        lax.all_to_all(
            output_rows.reshape(2, owners, piece_rows, width),
            "shard",
            split_axis=1,
            concat_axis=1,
            tiled=True,
        )
    )
    grad_out = (
        lax.all_to_all(deal_rows(cotangent[0]), "shard", split_axis=1, concat_axis=1, tiled=True)
        .reshape(length, width)
        .astype(jnp.float32)
    )
    gain_back, qkv_back, out_back, up_back, down_back = (
        gain,
        qkv_full,
        out_full,
        up_full,
        down_full,
    )
    grad_gate = jnp.sum(grad_out * result, axis=0)
    grad_result = (gate * grad_out).astype(jnp.bfloat16)
    grad_down_bias = jnp.sum(grad_result, axis=0, dtype=jnp.float32)
    grad_down_weight = inner_rows(hidden, grad_result)
    grad_hidden = times_transposed(grad_result, down_back)
    gelu_value, gelu_pull = jax.vjp(jax.nn.gelu, hidden_pre)
    grad_pre = gelu_pull(grad_hidden)[0].astype(jnp.bfloat16)
    grad_up_bias = jnp.sum(grad_pre, axis=0, dtype=jnp.float32)
    grad_up_weight = inner_rows(modulated, grad_pre)
    grad_modulated = times_transposed(grad_pre, up_back)
    grad_scale = jnp.sum(grad_modulated * normed_second, axis=0)
    grad_shift = jnp.sum(grad_modulated, axis=0)
    grad_middle = grad_out + normalize_back(
        grad_modulated * (1.0 + scale), normed_second, inverse_second
    )
    grad_modulation = jnp.concatenate([grad_shift, grad_scale, grad_gate])
    grad_ada_weight = features[:, None] * grad_modulation[None, :]
    grad_branch = grad_middle.astype(jnp.bfloat16)
    grad_out_bias = jnp.sum(grad_branch, axis=0, dtype=jnp.float32)
    grad_out_weight = inner_rows(attended, grad_branch)
    grad_attended = (
        times_transposed(grad_branch, out_back)
        .astype(jnp.bfloat16)
        .reshape(length, head_count, head_dim)
        .transpose(1, 0, 2)
    )

    def attend_back(items):
        query_head, key_head, value_head, grad_head, total_head = items
        grad_keys = jnp.zeros((length, head_dim), jnp.float32)
        grad_values = jnp.zeros((length, head_dim), jnp.float32)
        grad_queries = []
        for offset in range(0, length, block_rows):
            query_block = query_head[offset : offset + block_rows]
            grad_block = grad_head[offset : offset + block_rows]
            scores = (
                jnp.einsum("qd,kd->qk", query_block, key_head, preferred_element_type=jnp.float32)
                * factor
            )
            scores = jnp.where(key_live[None, :], scores, NEGATIVE)
            probs = jnp.exp(scores - total_head[offset : offset + block_rows][:, None])
            probs_low = probs.astype(jnp.bfloat16)
            grad_probs = jnp.einsum(
                "qd,kd->qk", grad_block, value_head, preferred_element_type=jnp.float32
            )
            row_terms = jnp.sum(probs * grad_probs, axis=1, keepdims=True)
            grad_scores = (probs * (grad_probs - row_terms)).astype(jnp.bfloat16)
            grad_values = grad_values + jnp.einsum(
                "qk,qd->kd", probs_low, grad_block, preferred_element_type=jnp.float32
            )
            grad_queries.append(
                jnp.dot(grad_scores, key_head, preferred_element_type=jnp.float32) * factor
            )
            grad_keys = (
                grad_keys
                + jnp.einsum(
                    "qk,qd->kd", grad_scores, query_block, preferred_element_type=jnp.float32
                )
                * factor
            )
        return (jnp.concatenate(grad_queries, axis=0), grad_keys, grad_values)

    grad_queries, grad_keys, grad_values = lax.map(
        attend_back, (queries, key_rows, value_rows, grad_attended, log_totals)
    )
    grad_queries = unrotate(grad_queries.transpose(1, 0, 2), cosines, sines).reshape(length, width)
    grad_keys = unrotate(grad_keys.transpose(1, 0, 2), cosines, sines).reshape(length, width)
    grad_values = grad_values.transpose(1, 0, 2).reshape(length, width)
    grad_projected = jnp.concatenate([grad_queries, grad_keys, grad_values], axis=1).astype(
        jnp.bfloat16
    )
    grad_qkv_bias = jnp.sum(grad_projected, axis=0, dtype=jnp.float32)
    grad_qkv_weight = inner_rows(normed_in, grad_projected)
    grad_normed = times_transposed(grad_projected, qkv_back)
    grad_ln_gain = jnp.sum(grad_normed * normed_first, axis=0)
    grad_ln_bias = jnp.sum(grad_normed, axis=0)
    grad_rows = grad_middle + normalize_back(grad_normed * gain_back, normed_first, inverse_first)
    grad_tokens = collect_rows(
        lax.all_to_all(
            grad_rows.astype(jnp.bfloat16).reshape(2, owners, piece_rows, width),
            "shard",
            split_axis=1,
            concat_axis=1,
            tiled=True,
        )
    )
    (
        owner_gain,
        owner_shift,
        owner_qkv,
        owner_qkv_bias,
        owner_out,
        owner_out_bias,
        owner_ada,
        owner_ada_bias,
        owner_up,
        owner_up_bias,
        owner_down,
        owner_down_bias,
    ) = (
        lax.psum_scatter(
            grad_ln_gain.astype(jnp.bfloat16), "shard", scatter_dimension=0, tiled=True
        ).astype(jnp.float32),
        lax.psum_scatter(
            grad_ln_bias.astype(jnp.bfloat16), "shard", scatter_dimension=0, tiled=True
        ).astype(jnp.float32),
        lax.psum_scatter(
            grad_qkv_weight.astype(jnp.bfloat16), "shard", scatter_dimension=0, tiled=True
        ).astype(jnp.float32),
        lax.psum_scatter(
            grad_qkv_bias.astype(jnp.bfloat16), "shard", scatter_dimension=0, tiled=True
        ).astype(jnp.float32),
        lax.psum_scatter(
            grad_out_weight.astype(jnp.bfloat16), "shard", scatter_dimension=0, tiled=True
        ).astype(jnp.float32),
        lax.psum_scatter(
            grad_out_bias.astype(jnp.bfloat16), "shard", scatter_dimension=0, tiled=True
        ).astype(jnp.float32),
        lax.psum_scatter(
            grad_ada_weight.astype(jnp.bfloat16), "shard", scatter_dimension=0, tiled=True
        ).astype(jnp.float32),
        lax.psum_scatter(
            grad_modulation.astype(jnp.bfloat16), "shard", scatter_dimension=0, tiled=True
        ).astype(jnp.float32),
        lax.psum_scatter(
            grad_up_weight.astype(jnp.bfloat16), "shard", scatter_dimension=0, tiled=True
        ).astype(jnp.float32),
        lax.psum_scatter(
            grad_up_bias.astype(jnp.bfloat16), "shard", scatter_dimension=0, tiled=True
        ).astype(jnp.float32),
        lax.psum_scatter(
            grad_down_weight.astype(jnp.bfloat16), "shard", scatter_dimension=0, tiled=True
        ).astype(jnp.float32),
        lax.psum_scatter(
            grad_down_bias.astype(jnp.bfloat16), "shard", scatter_dimension=0, tiled=True
        ).astype(jnp.float32),
    )
    summed = (
        lax.psum(owner_gain.astype(jnp.bfloat16), "replica").astype(jnp.float32),
        lax.psum(owner_shift.astype(jnp.bfloat16), "replica").astype(jnp.float32),
        lax.psum(owner_qkv.astype(jnp.bfloat16), "replica").astype(jnp.float32),
        lax.psum(owner_qkv_bias.astype(jnp.bfloat16), "replica").astype(jnp.float32),
        lax.psum(owner_out.astype(jnp.bfloat16), "replica").astype(jnp.float32),
        lax.psum(owner_out_bias.astype(jnp.bfloat16), "replica").astype(jnp.float32),
        lax.psum(owner_ada.astype(jnp.bfloat16), "replica").astype(jnp.float32),
        lax.psum(owner_ada_bias.astype(jnp.bfloat16), "replica").astype(jnp.float32),
        lax.psum(owner_up.astype(jnp.bfloat16), "replica").astype(jnp.float32),
        lax.psum(owner_up_bias.astype(jnp.bfloat16), "replica").astype(jnp.float32),
        lax.psum(owner_down.astype(jnp.bfloat16), "replica").astype(jnp.float32),
        lax.psum(owner_down_bias.astype(jnp.bfloat16), "replica").astype(jnp.float32),
    )
    return (mixed, held, grad_tokens) + tuple(summed)


def solution(mesh):
    placed = (
        P("replica", None, "shard", None),
        P("replica", None, "shard", None),
        P("replica", None),
        P("replica", None),
        P("replica", None),
        P("shard"),
        P("shard"),
        P("shard", None),
        P("shard"),
        P("shard", None),
        P("shard"),
        P("shard", None),
        P("shard"),
        P("shard", None),
        P("shard"),
        P("shard", None),
        P("shard"),
    )
    return jax.shard_map(
        on_device,
        mesh=mesh,
        in_specs=placed,
        out_specs=(
            P("replica", None, "shard", None),
            P("replica", "shard", None, None),
            P("replica", None, "shard", None),
            P("shard"),
            P("shard"),
            P("shard", None),
            P("shard"),
            P("shard", None),
            P("shard"),
            P("shard", None),
            P("shard"),
            P("shard", None),
            P("shard"),
            P("shard", None),
            P("shard"),
        ),
        check_vma=False,
    )
```

profile of v0, /device:TPU:0, one launch (start us, length us, event | category | flops | bytes accessed | tf_op | source)
XLA Modules:
  0.0 928.6 jit_solution(2725685308059135079)
XLA Ops:
  20.1 36.3 %all-gather = bf16[2,1,384]{2,1,0:T(2,128)(2,1)S(1)} all-gather(bf16[1,1,384]{2,1,0:T(2,128)(2,1)S(1)} %reshape.304), channel_id=1, replica_groups=mesh['replica'=16,'shard'=2] {'shard'}, dimensions={0}, use_global_device_ids=true | all-gather | bytes 2304 | tf_op jit(solution)/shard_map/all_gather | solution.py:151
  71.9 12.1 %all_gather.42 = bf16[128,2304]{1,0:T(8,128)(2,1)} all-gather(bf16[64,2304]{1,0:T(8,128)(2,1)S(1)} %copy-done.24), channel_id=1, replica_groups=mesh['replica'=16,'shard'=2] {'shard'}, dimensions={0}, use_global_device_ids=true | all-gather | bytes 884736 | tf_op jit(solution)/shard_map/all_gather | solution.py:157
  105.2 4.6 all-to-all-start.2
  112.0 18.3 %all-to-all-done.2 = bf16[2,2,256,768]{3,2,0,1:T(8,128)(2,1)} async-done(((bf16[2,2,256,768]{3,2,0,1:T(8,128)(2,1)}), bf16[2,2,256,768]{3,2,0,1:T(8,128)(2,1)}, u32[]{:S(2)}, u32[]{:S(2)}) %all-to-all-start.2) | async-done | bytes 1572896 | tf_op jit(solution)/shard_map/all_to_all | solution.py:239
  134.4 6.4 convolution_add_fusion.2
  163.5 116.5 %while.30 = (s32[]{:T(128)}, bf16[12,1024,64]{1,2,0:T(8,128)(2,1)}, f32[12,1024]{1,0:T(8,128)S(1)}, bf16[12,1024,64]{2,1,0:T(8,128)(2,1)}, bf16[12,1024,64]{2,1,...) while((s32[]{:T(128)}, bf16[12,1024,64]{1,2,0:T(8,128)(2,1)}, ...), condition=%wide.region_11.12_spmd.clone.clone, body=%wide.region_6.11_spmd.clone.sunk.clone | while | flops 281281536 | bytes 31123100 | solution.py:206
  284.4 14.2 %multiply_convert_fusion.2 = (bf16[1024,3072]{1,0:T(8,128)(2,1)}, f32[1024,3072]{1,0:T(8,128)}) fusion(f32[3072]{0:T(1024)S(1)} %bitcast.358, bf16[768,3072]{1,0:T(8,128)(2,1)} %all-gather.16.cloned.1.call-done, f32[1024,768]{1,0:T(8,128)S(1)} %get-tuple-element.423, f32[768]{0:T(1024)S(1)} %get-tuple-element.415, f32[768]{0:T(1024)S(1)} %get-tuple-element.416, ...), kind=kOutput, calls=%fused_computation.100 | convolution fusion | flops 4867227648 | bytes 26765312 | tf_op jit(solution)/shard_map/dot_general | solution.py:224
  298.6 11.8 %fusion.71 = (f32[768]{0:T(1024)S(1)}, bf16[1024,768]{1,0:T(8,128)(2,1)}, f32[1024,768]{1,0:T(8,128)}) fusion(f32[2,2,256,768]{3,2,1,0:T(8,128)} %copy.149, f32[768]{0:T(1024)S(1)} %reshape.324, f32[768]{0:T(1024)S(1)} %get-tuple-element.414, bf16[1024,3072]{1,0:T(8,128)(2,1)} %get-tuple-element.424, bf16[3072,768]{1,0:T(8,128)(2,1)} %all-gather.18.cloned.1.call-done), kind=kOutput, calls=%fused_computation.111 | convolution fusion | flops 4835769344 | bytes 18883584 | tf_op jit(solution)/shard_map/dot_general | solution.py:226
  310.4 14.7 %fusion.121 = (bf16[3072]{0:T(1024)(128)(2,1)S(1)}, bf16[1024,3072]{1,0:T(8,128)(2,1)S(1)}) fusion(f32[1024,3072]{1,0:T(8,128)} %get-tuple-element.425, f32[3072]{0:T(1024)S(1)} %bitcast.359, bf16[1024,768]{1,0:T(8,128)(2,1)} %get-tuple-element.405, bf16[3072,768]{1,0:T(8,128)(2,1)S(1)} %copy-done.42), kind=kOutput, calls=%fused_computation.222 | convolution fusion | flops 4901041152 | bytes 25184256 | tf_op jit(solution)/shard_map/dot_general | solution.py:70
  325.2 7.3 multiply_reduce_fusion.2
  333.5 5.9 convert_reduce_fusion.7
  350.1 206.9 %while.31 = (s32[]{:T(128)}, f32[12,1024,64]{1,2,0:T(8,128)}, f32[12,1024,64]{1,2,0:T(8,128)}, bf16[12,1024,64]{1,2,0:T(8,128)(2,1)}, bf16[12,1024,64]{2,1,0:T(8...) while((s32[]{:T(128)}, f32[12,1024,64]{1,2,0:T(8,128)}, ...), condition=%wide.region_20.21_spmd.clone.clone, body=%wide.region_17.20_spmd.clone.sunk.clone | while | flops 680853504 | bytes 36470412 | solution.py:312
  564.0 8.4 convolution_convert_fusion.2
  573.8 9.6 %convolution_convert_fusion = bf16[3072,768]{1,0:T(8,128)(2,1)} fusion(bf16[1024,3072]{1,0:T(8,128)(2,1)} %get-tuple-element.424, bf16[1024,768]{1,0:T(8,128)(2,1)S(1)} %copy-done.51), kind=kOutput, calls=%fused_computation.102 | convolution fusion | flops 4834197504 | bytes 12582912 | tf_op jit(solution)/shard_map/dot_general | solution.py:64
  583.5 10.7 %convolution_convert_fusion.1 = bf16[768,3072]{1,0:T(8,128)(2,1)} fusion(bf16[1024,3072]{1,0:T(8,128)(2,1)} %copy-done.50, f32[1024,768]{1,0:T(8,128)} %copy-done.6, f32[768]{0:T(1024)S(1)} %get-tuple-element.415, f32[768]{0:T(1024)S(1)} %get-tuple-element.416, f32[1024]{0:T(1024)S(1)} %add_rsqrt_fusion, f32[1024]{0:T(1024)S(1)} %broadcast_multiply_fusion.4), kind=kOutput, calls=%fused_computation.103 | convolution fusion | flops 4838129664 | bytes 14170112 | tf_op jit(solution)/shard_map/dot_general | solution.py:64
  594.4 30.2 %reduce-scatter.6.cloned.1.call-done = bf16[384,2304]{1,0:T(8,128)(2,1)} async-done(((bf16[768,2304]{1,0:T(8,128)(2,1)}), bf16[384,2304]{1,0:T(8,128)(2,1)}) %reduce-scatter.6.cloned.1.call-update) | async-done | bytes 1769488 | tf_op jit(solution)/shard_map/reduce_scatter | solution.py:356
  624.5 63.0 %reduce-scatter.14.cloned.1.call-done = bf16[1536,768]{1,0:T(8,128)(2,1)} async-done(((bf16[3072,768]{1,0:T(8,128)(2,1)}), bf16[1536,768]{1,0:T(8,128)(2,1)}) %reduce-scatter.14.cloned.1.call-update) | async-done | bytes 2359312 | tf_op jit(solution)/shard_map/reduce_scatter | solution.py:380
  687.5 63.0 %reduce-scatter.12.cloned.1.call-done = bf16[384,3072]{1,0:T(8,128)(2,1)} async-done(((bf16[768,3072]{1,0:T(8,128)(2,1)}), bf16[384,3072]{1,0:T(8,128)(2,1)}) %reduce-scatter.12.cloned.1.call-update) | async-done | bytes 2359312 | tf_op jit(solution)/shard_map/reduce_scatter | solution.py:374
  751.9 7.9 fusion.86
  763.9 4.8 all-to-all-start.3
  775.8 12.3 %all-to-all-done.3 = bf16[2,2,256,768]{3,0,2,1:T(2,128)(2,1)} async-done(((bf16[2,2,256,768]{3,0,2,1:T(2,128)(2,1)}), bf16[2,2,256,768]{3,0,2,1:T(2,128)(2,1)}, u32[]{:S(2)}, u32[]{:S(2)}) %all-to-all-start.3) | async-done | bytes 1572896 | tf_op jit(solution)/shard_map/all_to_all | solution.py:328
  794.8 18.9 %all-reduce.9 = (bf16[768]{0:T(1024)(128)(2,1)S(1)}, bf16[768]{0:T(1024)(128)(2,1)S(1)}, bf16[2304]{0:T(1024)(128)(2,1)S(1)}, bf16[768]{0:T(1024)(128)(2,1)S(1)}...) all-reduce(bf16[768]{0:T(1024)(128)(2,1)S(1)} %get-tuple-element.31, ...), channel_id=2, replica_groups=mesh['replica'=16,'shard'=2] {'shard'}, use_global_device_ids=true, to_apply=%region_24.25.clone | all-reduce | flops 10752 | bytes 43008
  814.2 60.7 %all-reduce.7 = (bf16[384]{0:T(512)(128)(2,1)S(1)}, bf16[384]{0:T(512)(128)(2,1)S(1)}, bf16[1152]{0:T(1024)(128)(2,1)S(1)}, bf16[384]{0:T(512)(128)(2,1)S(1)}, b...) all-reduce(bf16[384]{0:T(512)(128)(2,1)S(1)} %dynamic-slice.1, ...), channel_id=1, replica_groups=mesh['replica'=16,'shard'=2] {'replica'}, use_global_device_ids=true, to_apply=%region_25.26 | all-reduce | flops 5376 | bytes 21504 | tf_op jit(solution)/shard_map/psum | solution.py:388
  889.8 20.4 %all-reduce.12.cloned.1.call-done = (bf16[384,2304]{1,0:T(8,128)(2,1)}, bf16[384,768]{1,0:T(8,128)(2,1)}, bf16[64,2304]{1,0:T(8,128)(2,1)}, bf16[384,3072]{1,0:T(8,128)(2,1)}, bf16[1536,768]{1,0:T(8,128)(2,1)}) async-done(((bf16[384,2304]{1,0:T(8,128)(2,1)}, bf16[384,768]{1,0:T(8,128)(2,1)}, bf16[64,2304]{1,0:T(8,128)(2,1)}, bf16[384,3072]{1,0:T(8,128)(2,1)}, bf16[1536,768]{1,0:T(8,128)(2,1)}), ...) | async-done | bytes 7372816 | tf_op jit(solution)/shard_map/psum | solution.py:390
  (596 shorter events, 467.1 us)
Async XLA Ops:
  7.2 127.1 %all-gather.12.cloned.1.call-start = ((), (), s32[]{:S(2)}) async-start(), calls=%async_computation.9 | async-start | bytes 5308416 | tf_op jit(solution)/shard_map/all_gather | solution.py:153
  8.0 272.0 %all-gather.14.cloned.1.call-start = ((), (), s32[]{:S(2)}) async-start(), calls=%async_computation.10 | async-start | bytes 1769472 | tf_op jit(solution)/shard_map/all_gather | solution.py:155
  8.7 275.7 %all-gather.16.cloned.1.call-start = ((), (), s32[]{:S(2)}) async-start(), calls=%async_computation.11 | async-start | bytes 7077888 | tf_op jit(solution)/shard_map/all_gather | solution.py:159
  14.8 90.3 %all-to-all-start = ((bf16[2,2,256,768]{3,2,0,1:T(8,128)(2,1)}), bf16[2,2,256,768]{3,2,0,1:T(8,128)(2,1)S(1)}, u32[]{:S(2)}, u32[]{:S(2)}) async-start(bf16[2,2,256,768]{3,2,0,1:T(8,128)(2,1)} %copy.132), calls=%async_computation | async-start | bytes 3145728 | tf_op jit(solution)/shard_map/all_to_all | solution.py:133
  19.2 52.7 %copy-start.24 = (bf16[64,2304]{1,0:T(8,128)(2,1)S(1)}, bf16[64,2304]{1,0:T(8,128)(2,1)}, u32[]{:S(2)}) copy-start(bf16[64,2304]{1,0:T(8,128)(2,1)} %param.32) | copy-start | bytes 884740
  19.2 279.4 %all-gather.18.cloned.1.call-start = ((), (), s32[]{:S(2)}) async-start(), calls=%async_computation.12 | async-start | bytes 7077888 | tf_op jit(solution)/shard_map/all_gather | solution.py:161
  19.8 64.2 %copy-start.33 = (bf16[1152]{0:T(1024)(128)(2,1)S(1)}, bf16[1152]{0:T(1024)(128)(2,1)}, u32[]{:S(2)}) copy-start(bf16[1152]{0:T(1024)(128)(2,1)} %param.33) | copy-start | bytes 6916
  19.8 68.6 %copy-start.34 = (bf16[1536]{0:T(1024)(128)(2,1)S(1)}, bf16[1536]{0:T(1024)(128)(2,1)}, u32[]{:S(2)}) copy-start(bf16[1536]{0:T(1024)(128)(2,1)} %param.35) | copy-start | bytes 9220
  20.0 85.1 %copy-start.4 = (bf16[12,1024,64]{1,2,0:T(8,128)(2,1)}, bf16[12,1024,64]{1,2,0:T(8,128)(2,1)S(1)}, u32[]{:S(2)}) copy-start(bf16[12,1024,64]{1,2,0:T(8,128)(2,1)S(1)} %fusion.118) | copy-start | bytes 4718596
  56.4 77.3 %copy-start.26 = (f32[768]{0:T(1024)}, f32[768]{0:T(1024)S(1)}, u32[]{:S(2)}) copy-start(f32[768]{0:T(1024)S(1)} %reshape.318) | copy-start | bytes 9220
  105.2 25.2 %all-to-all-start.2 = ((bf16[2,2,256,768]{3,2,0,1:T(8,128)(2,1)}), bf16[2,2,256,768]{3,2,0,1:T(8,128)(2,1)}, u32[]{:S(2)}, u32[]{:S(2)}) async-start(bf16[2,2,256,768]{3,2,0,1:T(8,128)(2,1)} %copy.148), calls=%async_computation.2 | async-start | bytes 3145728 | tf_op jit(solution)/shard_map/all_to_all | solution.py:239
  109.8 484.5 %reduce-scatter.10.cloned.1.call-start = ((), (), s32[]{:S(2)}) async-start(), calls=%async_computation.15 | async-start | bytes 884736 | tf_op jit(solution)/shard_map/reduce_scatter | solution.py:368
  283.8 49.6 %copy-start.6 = (f32[1024,768]{1,0:T(8,128)}, f32[1024,768]{1,0:T(8,128)S(1)}, u32[]{:S(2)}) copy-start(f32[1024,768]{1,0:T(8,128)S(1)} %get-tuple-element.423) | copy-start | bytes 9437188
  333.4 260.9 %reduce-scatter.8.cloned.1.call-start = ((), (), s32[]{:S(2)}) async-start(), calls=%async_computation.14 | async-start | bytes 1769472 | tf_op jit(solution)/shard_map/reduce_scatter | solution.py:362
  350.1 274.4 %reduce-scatter.6.cloned.1.call-start = ((), (), s32[]{:S(2)}) async-start(), calls=%async_computation.13 | async-start | bytes 5308416 | tf_op jit(solution)/shard_map/reduce_scatter | solution.py:356
  350.1 207.0 %copy-start.20 = (f32[1024,32]{0,1:T(8,128)S(1)}, f32[1024,32]{0,1:T(8,128)}, u32[]{:S(2)}) copy-start(f32[1024,32]{0,1:T(8,128)} %copy-done.19) | copy-start | bytes 393220
  350.1 206.9 %copy-start.22 = (f32[1024,32]{0,1:T(8,128)S(1)}, f32[1024,32]{0,1:T(8,128)}, u32[]{:S(2)}) copy-start(f32[1024,32]{0,1:T(8,128)} %copy-done.21) | copy-start | bytes 393220
  572.4 115.1 %reduce-scatter.14.cloned.1.call-start = ((), (), s32[]{:S(2)}) async-start(), calls=%async_computation.17 | async-start | bytes 7077888 | tf_op jit(solution)/shard_map/reduce_scatter | solution.py:380
  583.4 167.0 %reduce-scatter.12.cloned.1.call-start = ((), (), s32[]{:S(2)}) async-start(), calls=%async_computation.16 | async-start | bytes 7077888 | tf_op jit(solution)/shard_map/reduce_scatter | solution.py:374
  594.3 315.9 %all-reduce.12.cloned.1.call-start = ((), (), s32[]{:S(2)}) async-start(), calls=%async_computation.18 | async-start | bytes 14745600 | tf_op jit(solution)/shard_map/psum | solution.py:390
  763.9 24.2 %all-to-all-start.3 = ((bf16[2,2,256,768]{3,0,2,1:T(2,128)(2,1)}), bf16[2,2,256,768]{3,0,2,1:T(2,128)(2,1)}, u32[]{:S(2)}, u32[]{:S(2)}) async-start(bf16[2,2,256,768]{3,0,2,1:T(2,128)(2,1)} %copy.154), calls=%async_computation.3 | async-start | bytes 3145728 | tf_op jit(solution)/shard_map/all_to_all | solution.py:328
  788.1 96.2 %all-to-all-start.1 = ((bf16[2,2,256,768]{3,0,2,1:T(2,128)(2,1)}), bf16[2,2,256,768]{3,0,2,1:T(2,128)(2,1)}, u32[]{:S(2)}, u32[]{:S(2)}) async-start(bf16[2,2,256,768]{3,0,2,1:T(2,128)(2,1)} %copy.144), calls=%async_computation.1 | async-start | bytes 3145728 | tf_op jit(solution)/shard_map/all_to_all | solution.py:230
  792.8 86.2 %copy-start.47 = (pred[2,2]{0,1:T(4,128)(4,1)S(1)}, pred[2,2]{0,1:T(4,128)(4,1)}, u32[]{:S(2)}) copy-start(pred[2,2]{0,1:T(4,128)(4,1)} %copy-done.46) | copy-start | bytes 16
  792.8 86.2 %copy-start.49 = (pred[2,2]{1,0:T(4,128)(4,1)S(1)}, pred[2,2]{1,0:T(4,128)(4,1)}, u32[]{:S(2)}) copy-start(pred[2,2]{1,0:T(4,128)(4,1)} %copy-done.48) | copy-start | bytes 16
  (66 other events, 509.6 us)
Sparse Core Ops, SparseCore 0:
  9.6 73.0 all-gather.11
  84.2 23.0 all-gather.13
  108.8 65.7 all-gather.15
  176.0 64.0 all-gather.17
  333.5 19.5 reduce-scatter.9
  355.8 21.8 reduce-scatter.7
  572.5 51.9 reduce-scatter.5
  627.4 60.0 reduce-scatter.13
  690.4 60.0 reduce-scatter.11
  754.6 155.5 all-reduce.11
where the time goes:
time: 940 us; the launch traced here: 929 us
  matrix products  390 us (41%)
  waiting for transfers between devices  210 us (22%)
  blocking collectives  155 us (16%)
  other arithmetic  70.4 us (7%)
  local copies, waits for them, and re-layouts  65.1 us (7%)
  starting transfers between devices  18.8 us (2%)
  between operations  18.7 us (2%)
    reduce_scatter x1, waiting for transfers between devices, on_device(): lax.psum_scatter(grad_up_weight.astype(jnp.bfloat16), 'shard', scatter_di...  63 us
    reduce_scatter x1, waiting for transfers between devices, on_device(): lax.psum_scatter(grad_down_weight.astype(jnp.bfloat16), 'shard', scatter_...  63 us
    psum x1, blocking collectives, on_device(): lax.psum(owner_gain.astype(jnp.bfloat16), 'replica').astype(jnp.float32)  60.7 us
    dot_general x24, matrix products, attend_back(): jnp.einsum('qd,kd->qk', query_block, key_head, preferred_element_type=jnp...  43.3 us
    dot_general x24, matrix products, attend(): jnp.einsum('qd,kd->qk', query_block, key_head, preferred_element_type=jnp...  42.1 us
    dot_general x24, matrix products, attend(): jnp.dot(probs, value_head, preferred_element_type=jnp.float32)  41.5 us
    dot_general x24, matrix products, attend_back(): jnp.einsum('qk,qd->kd', grad_scores, query_block, preferred_element_type=...  38.5 us
    dot_general x24, matrix products, attend_back(): jnp.einsum('qk,qd->kd', probs_low, grad_block, preferred_element_type=jnp...  37.9 us
  transfers between devices with their start and end apart: 14, of which 6 were waited for; matrix products, arithmetic and copies ran while one was open for 49% of the time, Pallas kernels for 0%

commit v1 on v0

--- a/solution.py
+++ b/solution.py
@@ -3,6 +3,8 @@
 import jax
 import jax.numpy as jnp
 from jax import lax
+from jax.experimental import pallas as pl
+from jax.experimental.pallas import tpu as pltpu
 from jax.sharding import PartitionSpec as P
 
 HEADS = 12
@@ -401,6 +403,447 @@
     return (mixed, held, grad_tokens) + tuple(summed)
 
 
+LANES = 128
+HEAD_DIM = 64
+LOW = jnp.bfloat16
+FULL = jnp.float32
+
+
+def partner(field):
+    lane = lax.broadcasted_iota(jnp.int32, field.shape, 1)
+    quarter = HEAD_DIM // 2
+    return jnp.where(
+        lane % HEAD_DIM < quarter,
+        pltpu.roll(field, LANES - quarter, 1),
+        pltpu.roll(field, quarter, 1),
+    )
+
+
+def one_head(field, head):
+    lane = lax.broadcasted_iota(jnp.int32, field.shape, 1)
+    return jnp.where(lane // HEAD_DIM == head, field, 0.0).astype(LOW)
+
+
+def attend_kernel(
+    q_ref,
+    k_ref,
+    v_ref,
+    far_k_ref,
+    far_v_ref,
+    cos_ref,
+    sin_ref,
+    out_ref,
+    q_turned_ref,
+    k_turned_ref,
+    v_low_ref,
+    total_ref,
+):
+    near = q_ref.shape[0]
+
+    def turn(field, start):
+        window = pl.ds(start, near)
+        return field * cos_ref[window, :] + partner(field) * sin_ref[window, :]
+
+    queries = turn(q_ref[...], 0).astype(LOW).astype(FULL) * (HEAD_DIM**-0.5)
+    q_turned_ref[...] = queries.astype(LOW)
+    k_turned_ref[pl.ds(0, near), :] = turn(k_ref[...], 0).astype(LOW)
+    k_turned_ref[pl.ds(near, near), :] = turn(far_k_ref[...], near).astype(LOW)
+    v_low_ref[pl.ds(0, near), :] = v_ref[...].astype(LOW)
+    v_low_ref[pl.ds(near, near), :] = far_v_ref[...].astype(LOW)
+    keys = k_turned_ref[...]
+    values_across = v_low_ref[...].T
+    outs = []
+    for head in range(LANES // HEAD_DIM):
+        scores = times_transposed(keys, one_head(queries, head))
+        highest = jnp.max(scores, axis=0, keepdims=True)
+        expon = jnp.exp(scores - highest)
+        summed = jnp.sum(expon, axis=0, keepdims=True)
+        across = jnp.dot(
+            values_across[head * HEAD_DIM : (head + 1) * HEAD_DIM],
+            expon.astype(LOW),
+            preferred_element_type=FULL,
+        )
+        outs.append(across / summed)
+        total_ref[0, head : head + 1, :] = highest + jnp.log(summed)
+    out_ref[...] = jnp.concatenate(outs, axis=0).T.astype(LOW)
+
+
+def attend(near_rows, far_rows, cosines, sines):
+    near = near_rows.shape[0]
+    pairs = near_rows.shape[1] // 3 // LANES
+    length = 2 * near
+    columns = pairs * LANES
+
+    def part(rows, first):
+        return pl.BlockSpec((rows, LANES), lambda pair, first=first: (0, first + pair))
+
+    whole = pl.BlockSpec((length, LANES), lambda pair: (0, 0))
+    return pl.pallas_call(
+        attend_kernel,
+        grid=(pairs,),
+        in_specs=[
+            part(near, 0),
+            part(near, pairs),
+            part(near, 2 * pairs),
+            part(near, 0),
+            part(near, pairs),
+            whole,
+            whole,
+        ],
+        out_specs=[
+            part(near, 0),
+            part(near, 0),
+            part(length, 0),
+            part(length, 0),
+            pl.BlockSpec((1, 8, near), lambda pair: (pair, 0, 0)),
+        ],
+        out_shape=[
+            jax.ShapeDtypeStruct((near, columns), LOW),
+            jax.ShapeDtypeStruct((near, columns), LOW),
+            jax.ShapeDtypeStruct((length, columns), LOW),
+            jax.ShapeDtypeStruct((length, columns), LOW),
+            jax.ShapeDtypeStruct((pairs, 8, near), FULL),
+        ],
+        cost_estimate=pl.CostEstimate(
+            flops=8 * near * length * columns,
+            bytes_accessed=4 * 5 * near * columns + 12 * near * columns,
+            transcendentals=near * length * 2 * pairs,
+        ),
+        name="attend",
+    )(near_rows, near_rows, near_rows, far_rows, far_rows, cosines, sines)
+
+
+def attend_back_kernel(
+    q_ref, k_ref, v_ref, grad_ref, total_ref, cos_ref, sin_ref, dq_ref, dk_ref, dv_ref
+):
+    near = q_ref.shape[0]
+    queries = q_ref[...].astype(FULL)
+    grads = grad_ref[...].astype(FULL)
+    keys = k_ref[...]
+    values = v_ref[...]
+    keys_across = keys.T
+    grad_keys = None
+    grad_values = None
+    grad_queries = []
+    for head in range(LANES // HEAD_DIM):
+        query_head = one_head(queries, head)
+        grad_head = one_head(grads, head)
+        scores = times_transposed(keys, query_head)
+        probs = jnp.exp(scores - total_ref[0, head : head + 1, :])
+        grad_probs = times_transposed(values, grad_head)
+        terms = jnp.sum(probs * grad_probs, axis=0, keepdims=True)
+        grad_scores = (probs * (grad_probs - terms)).astype(LOW)
+        value_part = jnp.dot(probs.astype(LOW), grad_head, preferred_element_type=FULL)
+        key_part = jnp.dot(grad_scores, query_head, preferred_element_type=FULL)
+        grad_values = value_part if grad_values is None else grad_values + value_part
+        grad_keys = key_part if grad_keys is None else grad_keys + key_part
+        grad_queries.append(
+            jnp.dot(
+                keys_across[head * HEAD_DIM : (head + 1) * HEAD_DIM],
+                grad_scores,
+                preferred_element_type=FULL,
+            )
+        )
+
+    def turn_back(field, rows):
+        return field * cos_ref[rows, :] - partner(field) * sin_ref[rows, :]
+
+    whole = pl.ds(0, 2 * near)
+    dq = jnp.concatenate(grad_queries, axis=0).T * (HEAD_DIM**-0.5)
+    dq_ref[...] = turn_back(dq, pl.ds(0, near)).astype(LOW)
+    dk_ref[...] = turn_back(grad_keys, whole).astype(LOW)
+    dv_ref[...] = grad_values.astype(LOW)
+
+
+def attend_back(queries, keys, values, grads, totals, cosines, sines):
+    near, columns = queries.shape
+    pairs = columns // LANES
+    length = 2 * near
+    row_part = pl.BlockSpec((near, LANES), lambda pair: (0, pair))
+    all_part = pl.BlockSpec((length, LANES), lambda pair: (0, pair))
+    whole = pl.BlockSpec((length, LANES), lambda pair: (0, 0))
+    return pl.pallas_call(
+        attend_back_kernel,
+        grid=(pairs,),
+        in_specs=[
+            row_part,
+            all_part,
+            all_part,
+            row_part,
+            pl.BlockSpec((1, 8, near), lambda pair: (pair, 0, 0)),
+            whole,
+            whole,
+        ],
+        out_specs=[row_part, all_part, all_part],
+        out_shape=[
+            jax.ShapeDtypeStruct((near, columns), LOW),
+            jax.ShapeDtypeStruct((length, columns), LOW),
+            jax.ShapeDtypeStruct((length, columns), LOW),
+        ],
+        cost_estimate=pl.CostEstimate(
+            flops=20 * near * length * columns,
+            bytes_accessed=2 * 11 * near * columns,
+            transcendentals=near * length * 2 * pairs,
+        ),
+        name="attend_back",
+    )(queries, keys, values, grads, totals, cosines, sines)
+
+
+def swap(array, axis, bit):
+    count = lax.axis_size(axis)
+    return lax.ppermute(array, axis, [(i, i ^ bit) for i in range(count)])
+
+
+def pick(array, index, dim=0):
+    return lax.dynamic_index_in_dim(array, index, dim, keepdims=False)
+
+
+def in_order(flag, mine, other, dim=0):
+    return jnp.where(
+        flag == 0, jnp.stack([mine, other], axis=dim), jnp.stack([other, mine], axis=dim)
+    )
+
+
+def replica_bits():
+    index = lax.axis_index("replica")
+    levels = lax.axis_size("replica").bit_length() - 1
+    return [(1 << level, (index >> level) % 2) for level in range(levels)]
+
+
+def fetch_other(local):
+    (core_bit, core), (side_bit, side) = replica_bits()[:2]
+    rows, columns = local.shape
+    quarter = pick(local.reshape(4, rows // 4, columns), side * 2 + core)
+    quarter = swap(quarter, "shard", 1)
+    half = in_order(side, quarter, swap(quarter, "replica", side_bit))
+    whole = in_order(core, half, swap(half, "replica", core_bit), 1)
+    return whole.reshape(rows, columns)
+
+
+def gather_rows(local, myself):
+    return in_order(myself, local, fetch_other(local)).reshape(
+        2 * local.shape[0], local.shape[1]
+    )
+
+
+def halve(blocks, flag, axis, bit, dim=0):
+    kept = pick(blocks, flag, dim)
+    sent = pick(blocks, 1 - flag, dim)
+    return (kept.astype(FULL) + swap(sent, axis, bit).astype(FULL)).astype(LOW)
+
+
+def reduce_rows(partial, myself):
+    columns = partial.shape[1]
+    bits = replica_bits()
+    part = halve(partial.reshape(2, 2, -1, columns), bits[0][1], "replica", 1, 1)
+    part = halve(part, myself, "shard", 1)
+    for bit, flag in bits[1:]:
+        part = halve(part.reshape(2, -1, columns), flag, "replica", bit)
+    for bit, flag in bits[::-1]:
+        part = in_order(flag, part, swap(part, "replica", bit)).reshape(-1, columns)
+    return part.astype(FULL)
+
+
+def on_half(
+    tokens,
+    cotangent,
+    seq_units,
+    deal,
+    timesteps,
+    ln_gain,
+    ln_bias,
+    qkv_weight,
+    qkv_bias,
+    out_weight,
+    out_bias,
+    ada_weight,
+    ada_bias,
+    up_weight,
+    up_bias,
+    down_weight,
+    down_bias,
+):
+    myself = lax.axis_index("shard")
+    unit_count, piece_rows, width = tokens.shape[1:]
+    near = unit_count * piece_rows
+    used = seq_units[0] > 0
+    owner = jnp.sum(jnp.where(used, deal[0], 0))
+    own_step = jnp.sum(jnp.where(used, timesteps[0], 0))
+
+    near_tokens = tokens[0].reshape(near, width)
+    qkv_full = gather_rows(qkv_weight, myself)
+    far_tokens = swap(near_tokens, "shard", 1)
+    vectors = (ln_gain, ln_bias, qkv_bias, out_bias, ada_bias, up_bias, down_bias)
+    packed = jnp.concatenate(vectors)
+    other_packed = swap(packed, "shard", 1)
+    gathered = []
+    offset = 0
+    for vector in vectors:
+        size = vector.shape[0]
+        gathered.append(
+            in_order(myself, vector, other_packed[offset : offset + size])
+            .reshape(-1)
+            .astype(FULL)
+        )
+        offset += size
+    gain, norm_shift, qkv_add, out_add, ada_add, up_add, down_add = gathered
+
+    ada_rows = ada_weight.shape[0]
+    features = time_features(own_step, 2 * ada_rows)
+    own_features = pick(features.reshape(2, ada_rows), myself)
+    modulation_part = jnp.dot(
+        own_features[None, :],
+        ada_weight.astype(FULL),
+        precision=HIGHEST,
+        preferred_element_type=FULL,
+    )[0]
+    modulation = modulation_part + swap(modulation_part, "shard", 1) + ada_add
+    shift = modulation[:width]
+    scale = modulation[width : 2 * width]
+    gate = modulation[2 * width :]
+
+    half = HEAD_DIM // 2
+    lane = jnp.arange(LANES)
+    freqs = jnp.exp(-math.log(10000.0) * (lane % half).astype(FULL) / half)
+    row = jnp.arange(2 * near)
+    holder = jnp.where(row < near, myself, 1 - myself)
+    inside = row % near
+    position = (inside // piece_rows) * (2 * piece_rows) + holder * piece_rows + inside % piece_rows
+    angles = position.astype(FULL)[:, None] * freqs[None, :]
+    cosines = jnp.cos(angles)
+    sines = jnp.where(lane % HEAD_DIM < half, -1.0, 1.0)[None, :] * jnp.sin(angles)
+
+    rows = near_tokens.astype(FULL)
+    near_normed, near_inverse = normalize(rows)
+    far_normed, far_inverse = normalize(far_tokens.astype(FULL))
+    near_in = (near_normed * gain + norm_shift).astype(LOW)
+    far_in = (far_normed * gain + norm_shift).astype(LOW)
+    near_rows = jnp.dot(near_in, qkv_full, preferred_element_type=FULL) + qkv_add
+    far_rows = (
+        jnp.dot(far_in, qkv_full[:, width:], preferred_element_type=FULL) + qkv_add[width:]
+    )
+    attended, queries, key_rows, value_rows, totals = attend(
+        near_rows, far_rows, cosines, sines
+    )
+
+    up_full = gather_rows(up_weight, myself)
+    down_full = gather_rows(down_weight, myself)
+    out_full = gather_rows(out_weight, myself)
+    middle = rows + jnp.dot(attended, out_full, preferred_element_type=FULL) + out_add
+    normed_second, inverse_second = normalize(middle)
+    modulated = (normed_second * (1.0 + scale) + shift).astype(LOW)
+    hidden_pre = jnp.dot(modulated, up_full, preferred_element_type=FULL) + up_add
+    hidden = jax.nn.gelu(hidden_pre).astype(LOW)
+    result = jnp.dot(hidden, down_full, preferred_element_type=FULL) + down_add
+    output_rows = (middle + gate * result).astype(LOW)
+    mixed = output_rows.reshape(1, unit_count, piece_rows, width)
+    own_output = output_rows.reshape(unit_count, piece_rows, width)
+    other_output = swap(own_output, "shard", 1)
+    held = in_order(myself, own_output, other_output, 1).reshape(2 * near, width)
+    held = jnp.where(owner == myself, held, jnp.zeros_like(held))[None, None]
+
+    grad_out = cotangent[0].reshape(near, width).astype(FULL)
+    grad_gate = jnp.sum(grad_out * result, axis=0)
+    grad_result = (gate * grad_out).astype(LOW)
+    grad_down_bias = jnp.sum(grad_result, axis=0, dtype=FULL)
+    grad_down_weight = inner_rows(hidden, grad_result).astype(LOW)
+    down_sum = reduce_rows(grad_down_weight, myself)
+    grad_hidden = times_transposed(grad_result, down_full)
+    gelu_pull = jax.vjp(jax.nn.gelu, hidden_pre)[1]
+    grad_pre = gelu_pull(grad_hidden)[0].astype(LOW)
+    grad_up_bias = jnp.sum(grad_pre, axis=0, dtype=FULL)
+    grad_up_weight = inner_rows(modulated, grad_pre).astype(LOW)
+    up_sum = reduce_rows(grad_up_weight, myself)
+    grad_modulated = times_transposed(grad_pre, up_full)
+    grad_scale = jnp.sum(grad_modulated * normed_second, axis=0)
+    grad_shift = jnp.sum(grad_modulated, axis=0)
+    grad_middle = grad_out + normalize_back(
+        grad_modulated * (1.0 + scale), normed_second, inverse_second
+    )
+    grad_branch = grad_middle.astype(LOW)
+    grad_out_bias = jnp.sum(grad_branch, axis=0, dtype=FULL)
+    grad_out_weight = inner_rows(attended, grad_branch).astype(LOW)
+    out_sum = reduce_rows(grad_out_weight, myself)
+    grad_attended = times_transposed(grad_branch, out_full).astype(LOW)
+
+    grad_modulation = jnp.concatenate([grad_shift, grad_scale, grad_gate])
+    note = jnp.concatenate([grad_modulation, jnp.full((LANES,), own_step.astype(FULL))])
+    notes = lax.all_gather(note, ("replica", "shard"), axis=0)
+    all_features = jax.vmap(lambda step: time_features(step, 2 * ada_rows))(
+        notes[:, 3 * width]
+    )
+    kept_features = pick(all_features.reshape(-1, 2, ada_rows), myself, 1)
+    all_modulation = notes[:, : 3 * width]
+    ada_sum = lax.dot_general(
+        kept_features,
+        all_modulation,
+        (((0,), (0,)), ((), ())),
+        precision=HIGHEST,
+        preferred_element_type=FULL,
+    )
+    ada_bias_sum = pick(jnp.sum(all_modulation, axis=0).reshape(2, -1), myself)
+    early = lax.psum(
+        jnp.concatenate([grad_down_bias, grad_up_bias, grad_out_bias]), ("replica", "shard")
+    )
+    hidden_units = grad_up_bias.shape[0]
+    down_bias_sum = pick(early[:width].reshape(2, -1), myself)
+    up_bias_sum = pick(early[width : width + hidden_units].reshape(2, -1), myself)
+    out_bias_sum = pick(early[width + hidden_units :].reshape(2, -1), myself)
+
+    grad_queries, grad_keys, grad_values = attend_back(
+        queries, key_rows, value_rows, grad_attended, totals, cosines, sines
+    )
+    both_in = jnp.concatenate([near_in, far_in], axis=0)
+    grad_qkv_weight = jnp.concatenate(
+        [
+            inner_rows(near_in, grad_queries).astype(LOW),
+            inner_rows(both_in, grad_keys).astype(LOW),
+            inner_rows(both_in, grad_values).astype(LOW),
+        ],
+        axis=1,
+    )
+    qkv_sum = reduce_rows(grad_qkv_weight, myself)
+    grad_qkv_bias = jnp.concatenate(
+        [jnp.sum(g, axis=0, dtype=FULL) for g in (grad_queries, grad_keys, grad_values)]
+    )
+    from_values = times_transposed(grad_values, qkv_full[:, 2 * width :])
+    from_keys = times_transposed(grad_keys, qkv_full[:, width : 2 * width])
+    from_queries = times_transposed(grad_queries, qkv_full[:, :width])
+    far_grad = from_values[near:] + from_keys[near:]
+    near_grad = from_values[:near] + from_keys[:near] + from_queries
+    far_back = normalize_back(far_grad * gain, far_normed, far_inverse).astype(LOW)
+    near_back = grad_middle + normalize_back(near_grad * gain, near_normed, near_inverse)
+    grad_rows = near_back + swap(far_back, "shard", 1).astype(FULL)
+    grad_tokens = grad_rows.astype(LOW).reshape(1, unit_count, piece_rows, width)
+    grad_ln_gain = jnp.sum(near_grad * near_normed, axis=0) + jnp.sum(
+        far_grad * far_normed, axis=0
+    )
+    grad_ln_bias = jnp.sum(near_grad, axis=0) + jnp.sum(far_grad, axis=0)
+    late = lax.psum(
+        jnp.concatenate([grad_ln_gain, grad_ln_bias, grad_qkv_bias]), ("replica", "shard")
+    )
+    gain_sum = pick(late[:width].reshape(2, -1), myself)
+    bias_sum = pick(late[width : 2 * width].reshape(2, -1), myself)
+    qkv_bias_sum = pick(late[2 * width :].reshape(2, -1), myself)
+    return (
+        mixed,
+        held,
+        grad_tokens,
+        gain_sum,
+        bias_sum,
+        qkv_sum,
+        qkv_bias_sum,
+        out_sum,
+        out_bias_sum,
+        ada_sum,
+        ada_bias_sum,
+        up_sum,
+        up_bias_sum,
+        down_sum,
+        down_bias_sum,
+    )
+
+
 def solution(mesh):
     placed = (
         P("replica", None, "shard", None),
@@ -421,8 +864,9 @@
         P("shard", None),
         P("shard"),
     )
+    halves = mesh.shape["shard"] == 2 and mesh.shape["replica"] in (4, 8, 16, 32)
     return jax.shard_map(
-        on_device,
+        on_half if halves else on_device,
         mesh=mesh,
         in_specs=placed,
         out_specs=(

time: 940 us -> 561 us (0.60)
  matrix products: 390 us -> 55.8 us
  blocking collectives: 155 us -> 107 us
  Pallas kernels: 0 us -> 41.7 us
  starting transfers between devices: 18.8 us -> 47.1 us
  local copies, waits for them, and re-layouts: 65.1 us -> 41.8 us
  waiting for transfers between devices: 210 us -> 191 us
  between operations: 18.7 us -> 4.11 us
    dot_general x177 -> x7, matrix products: 325 us -> 21.2 us  [the longest x1 6.02 us: on_half(): result = jnp.dot(hidden, down_full, preferred_element_type=FULL) + down_add]
    ppermute x0 -> x53, waiting for transfers between devices: none -> 191 us  [swap(): return lax.ppermute(array, axis, [(i, i ^ bit) for i in range(count)])]
    reduce_scatter x5 -> x0, waiting for transfers between devices: 156 us -> none  [the longest x1 63 us: on_device(): lax.psum_scatter(grad_up_weight.astype(jnp.bfloat16), 'shard', scatter_di...]
    ppermute x0 -> x53, starting transfers between devices: none -> 47.1 us  [swap(): return lax.ppermute(array, axis, [(i, i ^ bit) for i in range(count)])]
    pallas_call x0 -> x2, Pallas kernels: none -> 41.7 us  [the longest x1 24.6 us: attend_back(): pl.pallas_call(attend_back_kernel, grid=(pairs,), in_specs=[row_part, all...]
    all_to_all x4 -> x0, waiting for transfers between devices: 30.6 us -> none  [the longest x1 18.3 us: on_device(): lax.all_to_all(deal_rows(cotangent[0]), 'shard', split_axis=1, concat_axi...]
    psum x1, blocking collectives: 60.7 us -> 38.2 us  [on_half(): lax.psum(jnp.concatenate([grad_ln_gain, grad_ln_bias, grad_qkv_bias]), ('...]
    psum x1 -> x0, waiting for transfers between devices: 20.4 us -> none  [on_device(): lax.psum(owner_qkv.astype(jnp.bfloat16), 'replica').astype(jnp.float32)]
  transfers between devices with their start and end apart: 14 -> 53, of which waited for: 6 -> 27; matrix products, arithmetic and copies ran while one was open for 49% -> 18% of each run, Pallas kernels for 0% -> 3%
where the time goes in v1:
time: 561 us; the launch traced here: 552 us
  waiting for transfers between devices  191 us (34%)
  blocking collectives  107 us (19%)
  other arithmetic  63.4 us (11%)
  matrix products  55.8 us (10%)
  starting transfers between devices  47.1 us (8%)
  local copies, waits for them, and re-layouts  41.8 us (7%)
  Pallas kernels  41.7 us (7%)
    ppermute x53, waiting for transfers between devices, swap(): return lax.ppermute(array, axis, [(i, i ^ bit) for i in range(count)])  191 us
    all_gather x1, blocking collectives, on_half(): notes = lax.all_gather(note, ('replica', 'shard'), axis=0)  69.2 us
    ppermute x53, starting transfers between devices, swap(): return lax.ppermute(array, axis, [(i, i ^ bit) for i in range(count)])  47.1 us
    psum x1, blocking collectives, on_half(): lax.psum(jnp.concatenate([grad_ln_gain, grad_ln_bias, grad_qkv_bias]), ('...  38.2 us
    pallas_call x1, Pallas kernels, attend_back(): pl.pallas_call(attend_back_kernel, grid=(pairs,), in_specs=[row_part, all...  24.6 us
    dot_general x6, matrix products, times_transposed(): lax.dot_general(left, right, (((1,), (1,)), ((), ())), preferred_element_...  20.9 us
    select_n x32, other arithmetic, in_order(): jnp.where(flag == 0, jnp.stack([mine, other], axis=dim), jnp.stack([other...  17.5 us
    pallas_call x1, Pallas kernels, attend(): pl.pallas_call(attend_kernel, grid=(pairs,), in_specs=[part(near, 0), par...  17 us
  transfers between devices with their start and end apart: 53, of which 27 were waited for; matrix products, arithmetic and copies ran while one was open for 18% of the time, Pallas kernels for 3%

profile of v1, /device:TPU:0, one launch (start us, length us, event | category | flops | bytes accessed | tf_op | source)
XLA Modules:
  0.0 552.2 jit_solution(3048877988236342993)
XLA Ops:
  29.2 20.0 %collective-permute-done.8 = f32[2304]{0:T(1024)S(1)} collective-permute-done((f32[2304]{0:T(1024)S(1)}, f32[2304]{0:T(1024)S(1)}, u32[]{:S(2)}, u32[]{:S(2)}) %collective-permute-start.8) | collective-permute-done | bytes 9248 | tf_op jit(solution)/shard_map/ppermute | solution.py:594
  68.5 7.3 %collective-permute-done.2 = bf16[96,2304]{1,0:T(8,128)(2,1)S(1)} collective-permute-done((bf16[96,2304]{1,0:T(8,128)(2,1)S(1)}, bf16[96,2304]{1,0:T(8,128)(2,1)S(1)}, u32[]{:S(2)}, u32[]{:S(2)}) %collective-permute-start.2) | collective-permute-done | bytes 442400 | tf_op jit(solution)/shard_map/ppermute | solution.py:594
  76.2 12.3 %collective-permute-done.10 = bf16[96,3072]{1,0:T(8,128)(2,1)S(1)} collective-permute-done((bf16[96,3072]{1,0:T(8,128)(2,1)S(1)}, bf16[96,3072]{1,0:T(8,128)(2,1)S(1)}, u32[]{:S(2)}, u32[]{:S(2)}) %collective-permute-start.10) | collective-permute-done | bytes 589856 | tf_op jit(solution)/shard_map/ppermute | solution.py:594
  89.7 11.0 %collective-permute-done.13 = bf16[384,768]{1,0:T(8,128)(2,1)S(1)} collective-permute-done((bf16[384,768]{1,0:T(8,128)(2,1)S(1)}, bf16[384,768]{1,0:T(8,128)(2,1)S(1)}, u32[]{:S(2)}, u32[]{:S(2)}) %collective-permute-start.13) | collective-permute-done | bytes 589856 | tf_op jit(solution)/shard_map/ppermute | solution.py:594
  114.5 17.0 %attend.1 = (bf16[512,768]{1,0:T(8,128)(2,1)}, bf16[512,768]{1,0:T(8,128)(2,1)}, bf16[1024,768]{1,0:T(8,128)(2,1)}, bf16[1024,768]{1,0:T(8,128)(2,1)}, f32[6,8,512]{2,1,0:T(8,128)}) custom-call(f32[512,2304]{1,0:T(8,128)} %convolution_add_fusion.q_ref.k_ref.v_ref, f32[512,2304]{1,0:T(8,128)} %convolution_add_fusion.q_ref.k_ref.v_ref, ...), custom_call_target="tpu_custom_call" | custom-call | flops 3221225472 | bytes 12582912 | tf_op jit(solution)/shard_map/attend/pallas_call | solution.py:481
  144.2 7.2 %convert_reduce_fusion = (f32[3072]{0:T(1024)}, bf16[512,3072]{1,0:T(8,128)(2,1)S(1)}) fusion(f32[512,3072]{1,0:T(8,128)S(1)} %fusion.120, f32[3072]{0:T(1024)S(1)} %reshape.1325, bf16[512,768]{1,0:T(8,128)(2,1)S(1)} %bitcast.375, bf16[3072,768]{1,0:T(8,128)(2,1)S(1)} %bitcast.298), kind=kOutput, calls=%fused_computation.9 | convolution fusion | flops 2452091904 | bytes 14966784 | tf_op jit(solution)/shard_map/dot_general | solution.py:72
  154.5 4.9 convolution_convert_fusion.1
  159.5 6.0 %fusion.52 = (f32[768]{0:T(1024)S(1)}, bf16[512,768]{1,0:T(8,128)(2,1)}, f32[768]{0:T(1024)}, f32[512,768]{1,0:T(8,128)S(1)}, bf16[512,768]{1,0:T(8,128)(2,1)}) fusion(bf16[1,2,256,768]{3,2,1,0:T(8,128)(2,1)S(1)} %copy-done.28, f32[768]{0:T(1024)S(1)} %reshape.1326, f32[512,768]{1,0:T(8,128)S(1)} %get-tuple-element.87, f32[768]{0:T(1024)S(1)} %get-tuple-element.64, ...), kind=kOutput, calls=%fused_computation.98 | convolution fusion | flops 2439510528 | bytes 18123776 | tf_op jit(solution)/shard_map/dot_general | solution.py:737
  169.0 24.6 %attend_back.1 = (bf16[512,768]{1,0:T(8,128)(2,1)}, bf16[1024,768]{1,0:T(8,128)(2,1)}, bf16[1024,768]{1,0:T(8,128)(2,1)}) custom-call(bf16[512,768]{1,0:T(8,128)(2,1)} %get-tuple-element.24.q_ref, bf16[1024,768]{1,0:T(8,128)(2,1)} %get-tuple-element.25.k_ref, bf16[1024,768]{1,0:T(8,128)(2,1)} %get-tuple-element.26.v_ref, ...), custom_call_target="tpu_custom_call" | custom-call | flops 8053063680 | bytes 8650752 | tf_op jit(solution)/shard_map/attend_back/pallas_call | solution.py:565
  198.5 4.2 fusion.46
  217.7 69.2 %all-gather.1 = f32[32,1,2432]{2,1,0:T(1,128)S(1)} all-gather(f32[1,1,2432]{2,1,0:T(1,128)S(1)} %reshape.1353), channel_id=2, replica_groups=mesh['replica'=16,'shard'=2] {'replica','shard'}, dimensions={0}, use_global_device_ids=true | all-gather | bytes 321024 | tf_op jit(solution)/shard_map/all_gather | solution.py:771
  290.5 4.3 copy.42
  304.4 38.2 %all-reduce = (f32[3840]{0:T(1024)}, f32[4608]{0:T(1024)}) all-reduce(f32[3840]{0:T(1024)} %constant_dynamic-update-slice_fusion, f32[4608]{0:T(1024)} %pad_maximum_fusion.4), channel_id=1, replica_groups=mesh['replica'=16,'shard'=2] {'replica','shard'}, use_global_device_ids=true, to_apply=%region_21.22 | all-reduce | flops 8448 | bytes 67584 | tf_op jit(solution)/shard_map/psum | solution.py:822
  352.0 4.3 collective-permute-done.27
  391.2 13.6 %collective-permute-done.18 = bf16[192,2304]{1,0:T(8,128)(2,1)S(1)} collective-permute-done((bf16[192,2304]{1,0:T(8,128)(2,1)}, bf16[192,2304]{1,0:T(8,128)(2,1)S(1)}, u32[]{:S(2)}, u32[]{:S(2)}) %collective-permute-start.18) | collective-permute-done | bytes 884768 | tf_op jit(solution)/shard_map/ppermute | solution.py:594
  421.2 5.7 %collective-permute-done.21 = bf16[24,2304]{1,0:T(8,128)(2,1)S(1)} collective-permute-done((bf16[24,2304]{1,0:T(8,128)(2,1)S(1)}, bf16[24,2304]{1,0:T(8,128)(2,1)S(1)}, u32[]{:S(2)}, u32[]{:S(2)}) %collective-permute-start.21) | collective-permute-done | bytes 110624 | tf_op jit(solution)/shard_map/ppermute | solution.py:594
  427.0 19.9 %collective-permute-done.45 = bf16[768,768]{1,0:T(8,128)(2,1)S(1)} collective-permute-done((bf16[768,768]{1,0:T(8,128)(2,1)S(1)}, bf16[768,768]{1,0:T(8,128)(2,1)S(1)}, u32[]{:S(2)}, u32[]{:S(2)}) %collective-permute-start.45) | collective-permute-done | bytes 1179680 | tf_op jit(solution)/shard_map/ppermute | solution.py:594
  448.5 19.2 %collective-permute-done.36 = bf16[192,3072]{1,0:T(8,128)(2,1)S(1)} collective-permute-done((bf16[192,3072]{1,0:T(8,128)(2,1)S(1)}, bf16[192,3072]{1,0:T(8,128)(2,1)S(1)}, u32[]{:S(2)}, u32[]{:S(2)}) %collective-permute-start.36) | collective-permute-done | bytes 1179680 | tf_op jit(solution)/shard_map/ppermute | solution.py:594
  471.0 13.5 %collective-permute-done.37 = bf16[96,3072]{1,0:T(8,128)(2,1)S(1)} collective-permute-done((bf16[96,3072]{1,0:T(8,128)(2,1)S(1)}, bf16[96,3072]{1,0:T(8,128)(2,1)S(1)}, u32[]{:S(2)}, u32[]{:S(2)}) %collective-permute-start.37) | collective-permute-done | bytes 589856 | tf_op jit(solution)/shard_map/ppermute | solution.py:594
  487.0 7.5 %collective-permute-done.38 = bf16[48,3072]{1,0:T(8,128)(2,1)S(1)} collective-permute-done((bf16[48,3072]{1,0:T(8,128)(2,1)S(1)}, bf16[48,3072]{1,0:T(8,128)(2,1)S(1)}, u32[]{:S(2)}, u32[]{:S(2)}) %collective-permute-start.38) | collective-permute-done | bytes 294944 | tf_op jit(solution)/shard_map/ppermute | solution.py:594
  497.8 5.5 collective-permute-done.39
  512.0 4.4 collective-permute-done.50
  525.2 7.5 %collective-permute-done.51 = bf16[384,768]{1,0:T(8,128)(2,1)S(1)} collective-permute-done((bf16[384,768]{1,0:T(8,128)(2,1)S(1)}, bf16[384,768]{1,0:T(8,128)(2,1)S(1)}, u32[]{:S(2)}, u32[]{:S(2)}) %collective-permute-start.51) | collective-permute-done | bytes 589856 | tf_op jit(solution)/shard_map/ppermute | solution.py:594
  533.0 9.9 %collective-permute-done.42 = bf16[96,3072]{1,0:T(8,128)(2,1)S(1)} collective-permute-done((bf16[96,3072]{1,0:T(8,128)(2,1)S(1)}, bf16[96,3072]{1,0:T(8,128)(2,1)S(1)}, u32[]{:S(2)}, u32[]{:S(2)}) %collective-permute-start.42) | collective-permute-done | bytes 589856 | tf_op jit(solution)/shard_map/ppermute | solution.py:594
  (453 shorter events, 210.9 us)
Async XLA Ops:
  2.6 60.1 %collective-permute-start.1 = (bf16[96,2304]{1,0:T(8,128)(2,1)}, bf16[96,2304]{1,0:T(8,128)(2,1)S(1)}, u32[]{:S(2)}, u32[]{:S(2)}) collective-permute-start(bf16[96,2304]{1,0:T(8,128)(2,1)} %dynamic-slice_bitcast_fusion.12), channel_id=1, source_target_pairs={{0,1},{1,0},{2,3},{3,2},{4,5},{5,4},{6,7},{7,6},{8,9},{9,8},{10,11... | collective-permute-start | bytes 1327112 | tf_op jit(solution)/shard_map/ppermute | solution.py:594
  11.7 55.9 %collective-permute-start.4 = (bf16[512,768]{1,0:T(8,128)(2,1)}, bf16[512,768]{1,0:T(8,128)(2,1)S(1)}, u32[]{:S(2)}, u32[]{:S(2)}) collective-permute-start(bf16[512,768]{1,0:T(8,128)(2,1)} %bitcast.279), channel_id=1, source_target_pairs={{0,1},{1,0},{2,3},{3,2},{4,5},{5,4},{6,7},{7,6},{8,9},{9,8},{10,11... | collective-permute-start | bytes 2359304 | tf_op jit(solution)/shard_map/ppermute | solution.py:594
  15.3 37.6 %collective-permute-start.5 = (bf16[96,768]{1,0:T(8,128)(2,1)}, bf16[96,768]{1,0:T(8,128)(2,1)}, u32[]{:S(2)}, u32[]{:S(2)}) collective-permute-start(bf16[96,768]{1,0:T(8,128)(2,1)} %dynamic-slice_bitcast_fusion.20), channel_id=1, source_target_pairs={{0,1},{1,0},{2,3},{3,2},{4,5},{5,4},{6,7},{7,6},{8,9},{9,8},{10,11... | collective-permute-start | bytes 442376 | tf_op jit(solution)/shard_map/ppermute | solution.py:594
  17.3 47.0 %collective-permute-start.9 = (bf16[96,3072]{1,0:T(8,128)(2,1)}, bf16[96,3072]{1,0:T(8,128)(2,1)S(1)}, u32[]{:S(2)}, u32[]{:S(2)}) collective-permute-start(bf16[96,3072]{1,0:T(8,128)(2,1)} %dynamic-slice_bitcast_fusion.10), channel_id=1, source_target_pairs={{0,1},{1,0},{2,3},{3,2},{4,5},{5,4},{6,7},{7,6},{8,9},{9,8},{10,11... | collective-permute-start | bytes 1769480 | tf_op jit(solution)/shard_map/ppermute | solution.py:594
  64.3 24.2 %collective-permute-start.10 = (bf16[96,3072]{1,0:T(8,128)(2,1)S(1)}, bf16[96,3072]{1,0:T(8,128)(2,1)S(1)}, u32[]{:S(2)}, u32[]{:S(2)}) collective-permute-start(bf16[96,3072]{1,0:T(8,128)(2,1)S(1)} %collective-permute-done.9), channel_id=1, source_target_pairs={{0,4},{2,6},{4,0},{6,2},{8,12},{10,14},{12,8},{14,10},{16,20},{18,... | collective-permute-start | bytes 1769480 | tf_op jit(solution)/shard_map/ppermute | solution.py:594
  64.8 35.8 %collective-permute-start.13 = (bf16[384,768]{1,0:T(8,128)(2,1)S(1)}, bf16[384,768]{1,0:T(8,128)(2,1)S(1)}, u32[]{:S(2)}, u32[]{:S(2)}) collective-permute-start(bf16[384,768]{1,0:T(8,128)(2,1)S(1)} %collective-permute-done.12), channel_id=1, source_target_pairs={{0,4},{2,6},{4,0},{6,2},{8,12},{10,14},{12,8},{14,10},{16,20},{18,... | collective-permute-start | bytes 1769480 | tf_op jit(solution)/shard_map/ppermute | solution.py:594
  76.0 28.6 %collective-permute-start.3 = (bf16[2,96,2304]{2,1,0:T(8,128)(2,1)S(1)}, bf16[2,96,2304]{2,1,0:T(8,128)(2,1)S(1)}, u32[]{:S(2)}, u32[]{:S(2)}) collective-permute-start(bf16[2,96,2304]{2,1,0:T(8,128)(2,1)S(1)} %maximum_select_fusion.18), channel_id=1, source_target_pairs={{0,2},{2,0},{4,6},{6,4},{8,10},{10,8},{12,14},{14,12},{16,18},{18,... | collective-permute-start | bytes 2654216 | tf_op jit(solution)/shard_map/ppermute | solution.py:594
  89.7 44.6 %collective-permute-start.11 = (bf16[2,96,3072]{2,1,0:T(8,128)(2,1)}, bf16[2,96,3072]{2,1,0:T(8,128)(2,1)}, u32[]{:S(2)}, u32[]{:S(2)}) collective-permute-start(bf16[2,96,3072]{2,1,0:T(8,128)(2,1)} %maximum_select_fusion.12), channel_id=1, source_target_pairs={{0,2},{2,0},{4,6},{6,4},{8,10},{10,8},{12,14},{14,12},{16,18},{18,... | collective-permute-start | bytes 3538952 | tf_op jit(solution)/shard_map/ppermute | solution.py:594
  101.9 36.5 %collective-permute-start.14 = (bf16[2,384,768]{2,1,0:T(8,128)(2,1)}, bf16[2,384,768]{2,1,0:T(8,128)(2,1)}, u32[]{:S(2)}, u32[]{:S(2)}) collective-permute-start(bf16[2,384,768]{2,1,0:T(8,128)(2,1)} %maximum_select_fusion.14), channel_id=1, source_target_pairs={{0,2},{2,0},{4,6},{6,4},{8,10},{10,8},{12,14},{14,12},{16,18},{18,... | collective-permute-start | bytes 3538952 | tf_op jit(solution)/shard_map/ppermute | solution.py:594
  215.2 191.0 %collective-permute-start.44 = (bf16[2,768,768]{2,1,0:T(8,128)(2,1)}, bf16[2,768,768]{2,1,0:T(8,128)(2,1)}, u32[]{:S(2)}, u32[]{:S(2)}) collective-permute-start(bf16[2,768,768]{2,1,0:T(8,128)(2,1)} %dynamic-slice_bitcast_fusion), channel_id=1, source_target_pairs={{0,2},{2,0},{4,6},{6,4},{8,10},{10,8},{12,14},{14,12},{16,18},{18,... | collective-permute-start | bytes 7077896 | tf_op jit(solution)/shard_map/ppermute | solution.py:594
  217.3 196.4 %collective-permute-start.35 = (bf16[2,192,3072]{2,1,0:T(8,128)(2,1)}, bf16[2,192,3072]{2,1,0:T(8,128)(2,1)}, u32[]{:S(2)}, u32[]{:S(2)}) collective-permute-start(bf16[2,192,3072]{2,1,0:T(8,128)(2,1)} %dynamic-slice_bitcast_fusion.1), channel_id=1, source_target_pairs={{0,2},{2,0},{4,6},{6,4},{8,10},{10,8},{12,14},{14,12},{16,18},{18,... | collective-permute-start | bytes 7077896 | tf_op jit(solution)/shard_map/ppermute | solution.py:594
  288.5 58.3 %collective-permute-start.26 = (bf16[2,192,768]{2,1,0:T(8,128)(2,1)}, bf16[2,192,768]{2,1,0:T(8,128)(2,1)}, u32[]{:S(2)}, u32[]{:S(2)}) collective-permute-start(bf16[2,192,768]{2,1,0:T(8,128)(2,1)} %dynamic-slice_bitcast_fusion.8), channel_id=1, source_target_pairs={{0,2},{2,0},{4,6},{6,4},{8,10},{10,8},{12,14},{14,12},{16,18},{18,... | collective-permute-start | bytes 1769480 | tf_op jit(solution)/shard_map/ppermute | solution.py:594
  296.3 78.1 %collective-permute-start.17 = (bf16[2,192,2304]{2,1,0:T(8,128)(2,1)}, bf16[2,192,2304]{2,1,0:T(8,128)(2,1)}, u32[]{:S(2)}, u32[]{:S(2)}) collective-permute-start(bf16[2,192,2304]{2,1,0:T(8,128)(2,1)} %dynamic-slice_bitcast_fusion.2), channel_id=1, source_target_pairs={{0,2},{2,0},{4,6},{6,4},{8,10},{10,8},{12,14},{14,12},{16,18},{18,... | collective-permute-start | bytes 5308424 | tf_op jit(solution)/shard_map/ppermute | solution.py:594
  378.6 26.2 %collective-permute-start.18 = (bf16[192,2304]{1,0:T(8,128)(2,1)}, bf16[192,2304]{1,0:T(8,128)(2,1)S(1)}, u32[]{:S(2)}, u32[]{:S(2)}) collective-permute-start(bf16[192,2304]{1,0:T(8,128)(2,1)} %dynamic-slice_bitcast_fusion.5), channel_id=1, source_target_pairs={{0,1},{1,0},{2,3},{3,2},{4,5},{5,4},{6,7},{7,6},{8,9},{9,8},{10,11... | collective-permute-start | bytes 2654216 | tf_op jit(solution)/shard_map/ppermute | solution.py:594
  384.1 126.2 %collective-permute-start.15 = (bf16[2,256,768]{2,1,0:T(8,128)(2,1)}, bf16[2,256,768]{2,1,0:T(8,128)(2,1)S(1)}, u32[]{:S(2)}, u32[]{:S(2)}) collective-permute-start(bf16[2,256,768]{2,1,0:T(8,128)(2,1)} %bitcast.377), channel_id=1, source_target_pairs={{0,1},{1,0},{2,3},{3,2},{4,5},{5,4},{6,7},{7,6},{8,9},{9,8},{10,11... | collective-permute-start | bytes 2359304 | tf_op jit(solution)/shard_map/ppermute | solution.py:594
  391.1 120.8 %collective-permute-start.34 = (bf16[192,768]{1,0:T(8,128)(2,1)S(1)}, bf16[192,768]{1,0:T(8,128)(2,1)S(1)}, u32[]{:S(2)}, u32[]{:S(2)}) collective-permute-start(bf16[192,768]{1,0:T(8,128)(2,1)S(1)} %bitcast.360), channel_id=1, source_target_pairs={{0,2},{2,0},{4,6},{6,4},{8,10},{10,8},{12,14},{14,12},{16,18},{18,... | collective-permute-start | bytes 884744 | tf_op jit(solution)/shard_map/ppermute | solution.py:594
  409.4 37.5 %collective-permute-start.45 = (bf16[768,768]{1,0:T(8,128)(2,1)S(1)}, bf16[768,768]{1,0:T(8,128)(2,1)S(1)}, u32[]{:S(2)}, u32[]{:S(2)}) collective-permute-start(bf16[768,768]{1,0:T(8,128)(2,1)S(1)} %dynamic-slice_bitcast_fusion.3), channel_id=1, source_target_pairs={{0,1},{1,0},{2,3},{3,2},{4,5},{5,4},{6,7},{7,6},{8,9},{9,8},{10,11... | collective-permute-start | bytes 3538952 | tf_op jit(solution)/shard_map/ppermute | solution.py:594
  420.9 46.9 %collective-permute-start.36 = (bf16[192,3072]{1,0:T(8,128)(2,1)S(1)}, bf16[192,3072]{1,0:T(8,128)(2,1)S(1)}, u32[]{:S(2)}, u32[]{:S(2)}) collective-permute-start(bf16[192,3072]{1,0:T(8,128)(2,1)S(1)} %dynamic-slice_bitcast_fusion.4), channel_id=1, source_target_pairs={{0,1},{1,0},{2,3},{3,2},{4,5},{5,4},{6,7},{7,6},{8,9},{9,8},{10,11... | collective-permute-start | bytes 3538952 | tf_op jit(solution)/shard_map/ppermute | solution.py:594
  427.0 21.5 %collective-permute-start.22 = (bf16[24,2304]{1,0:T(8,128)(2,1)S(1)}, bf16[24,2304]{1,0:T(8,128)(2,1)S(1)}, u32[]{:S(2)}, u32[]{:S(2)}) collective-permute-start(bf16[24,2304]{1,0:T(8,128)(2,1)S(1)} %fusion.73), channel_id=1, source_target_pairs={{0,16},{2,18},{4,20},{6,22},{8,24},{10,26},{12,28},{14,30},{16,0},... | collective-permute-start | bytes 331784 | tf_op jit(solution)/shard_map/ppermute | solution.py:594
  447.3 23.2 %collective-permute-start.46 = (bf16[384,768]{1,0:T(8,128)(2,1)S(1)}, bf16[384,768]{1,0:T(8,128)(2,1)S(1)}, u32[]{:S(2)}, u32[]{:S(2)}) collective-permute-start(bf16[384,768]{1,0:T(8,128)(2,1)S(1)} %dynamic-slice_bitcast_fusion.6), channel_id=1, source_target_pairs={{0,4},{2,6},{4,0},{6,2},{8,12},{10,14},{12,8},{14,10},{16,20},{18,... | collective-permute-start | bytes 1769480 | tf_op jit(solution)/shard_map/ppermute | solution.py:594
  448.4 21.6 %collective-permute-start.23 = (bf16[48,2304]{1,0:T(8,128)(2,1)S(1)}, bf16[48,2304]{1,0:T(8,128)(2,1)S(1)}, u32[]{:S(2)}, u32[]{:S(2)}) collective-permute-start(bf16[48,2304]{1,0:T(8,128)(2,1)S(1)} %bitcast.368), channel_id=1, source_target_pairs={{0,8},{2,10},{4,12},{6,14},{8,0},{10,2},{12,4},{14,6},{16,24},{18,... | collective-permute-start | bytes 663560 | tf_op jit(solution)/shard_map/ppermute | solution.py:594
  470.1 33.3 %collective-permute-start.24 = (bf16[96,2304]{1,0:T(8,128)(2,1)S(1)}, bf16[96,2304]{1,0:T(8,128)(2,1)S(1)}, u32[]{:S(2)}, u32[]{:S(2)}) collective-permute-start(bf16[96,2304]{1,0:T(8,128)(2,1)S(1)} %bitcast.343), channel_id=1, source_target_pairs={{0,4},{2,6},{4,0},{6,2},{8,12},{10,14},{12,8},{14,10},{16,20},{18,... | collective-permute-start | bytes 1327112 | tf_op jit(solution)/shard_map/ppermute | solution.py:594
  503.5 21.4 %collective-permute-start.25 = (bf16[192,2304]{1,0:T(8,128)(2,1)S(1)}, bf16[192,2304]{1,0:T(8,128)(2,1)S(1)}, u32[]{:S(2)}, u32[]{:S(2)}) collective-permute-start(bf16[192,2304]{1,0:T(8,128)(2,1)S(1)} %bitcast.317), channel_id=1, source_target_pairs={{0,2},{2,0},{4,6},{6,4},{8,10},{10,8},{12,14},{14,12},{16,18},{18,... | collective-permute-start | bytes 2654216 | tf_op jit(solution)/shard_map/ppermute | solution.py:594
  522.0 21.0 %collective-permute-start.42 = (bf16[96,3072]{1,0:T(8,128)(2,1)S(1)}, bf16[96,3072]{1,0:T(8,128)(2,1)S(1)}, u32[]{:S(2)}, u32[]{:S(2)}) collective-permute-start(bf16[96,3072]{1,0:T(8,128)(2,1)S(1)} %bitcast.332), channel_id=1, source_target_pairs={{0,4},{2,6},{4,0},{6,2},{8,12},{10,14},{12,8},{14,10},{16,20},{18,... | collective-permute-start | bytes 1769480 | tf_op jit(solution)/shard_map/ppermute | solution.py:594
  (106 other events, 1458.4 us)
